TPU v7x, 128 devices: a whole 4x4x4 slice. The times are simulated.
128 devices in a mesh: layer: 8 (over y_hi, x), width: 16 (over y_lo, z, core).
Axes of the slice: x: 4, y: 4 (y_hi: 2, y_lo: 2; y = y_hi * 2 + y_lo), z: 4, core: 2. Of those that a mesh axis runs over, the one named last changes fastest.
Arguments:
- source: bfloat16 [8, 4096, 4096], P('layer', 'width'), may hold values from -6 to 6
- expand_out: bfloat16 [2560, 4096], P(None, 'width'), may hold values from -0.125 to 0.125
- expand_in: bfloat16 [2560, 4096], P(('layer', 'width')), may hold values from -0.09375 to 0.09375
- depth: float32 [16, 8], P('layer'), may hold values from -1.4 to 1.4
Outputs:
- grown: float32 [16, 2560, 2560], P('layer', 'width')
All inputs are finite; a program needn't handle non-finite values.
Results may differ from a plain program's by a relative error of at most 0.018.
Values may be sent and summed in bfloat16 or wider, within the bound.
A program may use at most 128 MiB of HBM per device.

v0:
```python
import jax
import jax.numpy as jnp
from jax import lax
from jax.sharding import Mesh
from jax.sharding import PartitionSpec as P

LAYER_WIDTH = ("layer_0", "layer_1", "width")
LAYER = ("layer_0", "layer_1")


def in_order(parts, dim):
    parts = jnp.moveaxis(parts, 0, dim)
    dims = parts.shape
    return parts.reshape(*dims[:dim], dims[dim] * dims[dim + 1], *dims[dim + 2 :])


def stacked_from(value, axes, order):
    parts = value[None]
    for k in order:
        parts = lax.all_gather(parts, axes[k], axis=0, tiled=True)
    current = [lax.axis_size(axes[k]) for k in reversed(order)]
    parts = parts.reshape(*current, *value.shape)
    turned = sorted(range(len(order)), key=lambda place: order[len(order) - 1 - place])
    return parts.transpose(*turned, *range(len(order), parts.ndim)).reshape(-1, *value.shape)


def gathered_by_axis(value, axes, order, dim):
    return in_order(stacked_from(value, axes, order), dim)


def on_device(source, expand_out, expand_in, depth):
    src_held, row_count, inner_width = source.shape
    stacked = source.reshape(src_held * row_count, inner_width)
    projected = lax.dot_general(
        stacked,
        lax.all_gather(expand_in, LAYER_WIDTH, axis=0, tiled=True),
        (((1,), (1,)), ((), ())),
        preferred_element_type=jnp.float32,
    )
    columns = projected.shape[1]
    projected = projected.astype(jnp.bfloat16).reshape(src_held, row_count, columns)
    own_rows = expand_out.shape[0] // lax.axis_size("width")
    partial_value = jnp.einsum(
        "ri,kic->rkc", expand_out, projected, preferred_element_type=jnp.float32
    ).astype(jnp.bfloat16)
    partial_value = lax.optimization_barrier(partial_value)
    summed = lax.psum_scatter(
        partial_value.astype(jnp.float32)
        .reshape(own_rows * lax.axis_size("width"), src_held * columns)
        .astype(jnp.bfloat16),
        "width",
        scatter_dimension=0,
        tiled=True,
    )
    expanded = summed.reshape(own_rows, src_held, columns)
    return jnp.einsum(
        "tm,rmc->trc",
        depth,
        gathered_by_axis(expanded, LAYER, (0, 1), 1).astype(jnp.float32),
        precision=lax.Precision.HIGHEST,
        preferred_element_type=jnp.float32,
    )


def solution(mesh):
    finer = Mesh(mesh.devices.reshape(2, 4, mesh.shape["width"]), ("layer_0", "layer_1", "width"))
    return jax.shard_map(
        on_device,
        mesh=finer,
        in_specs=(P(LAYER, "width", None), P(None, "width"), P(LAYER_WIDTH, None), P(LAYER, None)),
        out_specs=P(LAYER, "width", None),
        check_vma=False,
    )
```

profile of v0, /device:TPU:1, one launch (start us, length us, event | category | flops | bytes accessed | tf_op | source)
XLA Modules:
  0.0 518.2 jit_solution(15276849728186745125)
XLA Ops:
  6.5 0.0 copy-start
  6.5 0.0 all-gather.10.cloned.1.call-start
  6.5 0.7 all-gather.10.cloned.1.call-update
  7.3 0.0 copy-start.3
  7.3 0.0 reduce-scatter.4.cloned.1.call-start
  7.3 228.3 %all-gather.10.cloned.1.call-done = bf16[128,20,4096]{2,1,0:T(8,128)(2,1)} async-done(((bf16[1,20,4096]{2,1,0:T(8,128)(2,1)}), bf16[128,20,4096]{2,1,0:T(8,128)(2,1)}) %all-gather.10.cloned.1.call-update) | async-done | bytes 20971536 | tf_op jit(solution)/shard_map/all_gather | solution.py:36
  235.6 26.5 %reshape.25 = bf16[2560,4096]{1,0:T(8,128)(2,1)} reshape(bf16[128,20,4096]{2,1,0:T(8,128)(2,1)} %all-gather.10.cloned.1.call-done) | data formatting | bytes 41943040
  262.1 0.0 copy-done
  262.1 0.0 copy-done.3
  262.1 16.7 %fusion = bf16[2560,1,2560]{0,2,1:T(8,128)(2,1)} fusion(bf16[2560,256]{1,0:T(8,128)(2,1)S(1)} %copy-done.3, bf16[2560,4096]{1,0:T(8,128)(2,1)} %reshape.25, bf16[1,256,4096]{2,1,0:T(8,128)(2,1)S(1)} %copy-done), kind=kOutput, calls=%fused_computation.1 | convolution fusion | flops 8731361280 | bytes 37486592 | tf_op jit(solution)/shard_map/ri,kic->rkc/dot_general | solution.py:43
  278.8 17.6 %copy.14 = bf16[2560,2560]{1,0:T(8,128)(2,1)} copy(bf16[2560,2560]{0,1:T(8,128)(2,1)} %bitcast.34) | data formatting | bytes 26214400
  296.4 0.0 reduce-scatter.4.cloned.1.call-update
  296.5 0.0 all-gather.8.cloned.1.call-start
  296.5 79.2 %reduce-scatter.4.cloned.1.call-done = bf16[160,2560]{1,0:T(8,128)(2,1)} async-done(((bf16[2560,2560]{1,0:T(8,128)(2,1)}), bf16[160,2560]{1,0:T(8,128)(2,1)}) %reduce-scatter.4.cloned.1.call-update) | async-done | bytes 819216 | tf_op jit(solution)/shard_map/reduce_scatter | solution.py:47
  375.7 0.0 all-gather.8.cloned.1.call-update
  375.7 0.2 all-gather.6.cloned.1.call-start
  376.0 35.2 %all-gather.8.cloned.1.call-done = bf16[320,2560]{1,0:T(8,128)(2,1)} async-done(((bf16[160,2560]{1,0:T(8,128)(2,1)}), bf16[320,2560]{1,0:T(8,128)(2,1)}) %all-gather.8.cloned.1.call-update) | async-done | bytes 1638416 | tf_op jit(solution)/shard_map/all_gather | solution.py:20
  411.2 0.0 all-gather.6.cloned.1.call-update
  411.2 68.7 %all-gather.6.cloned.1.call-done = bf16[8,160,1,2560]{3,1,2,0:T(8,128)(2,1)} async-done(((bf16[2,160,1,2560]{3,1,2,0:T(8,128)(2,1)}), bf16[8,160,1,2560]{3,1,2,0:T(8,128)(2,1)}) %all-gather.6.cloned.1.call-update) | async-done | bytes 6553616 | tf_op jit(solution)/shard_map/all_gather | solution.py:20
  479.9 10.6 %copy.12 = bf16[2,4,160,1,2560]{4,1,0,2,3:T(4,128)(2,1)} copy(bf16[2,4,160,1,2560]{4,2,0,1,3:T(8,128)(2,1)} %bitcast.35) | data formatting | bytes 13107200 | tf_op jit(solution)/shard_map/transpose | solution.py:24
  490.5 0.0 copy-start.2
  490.5 0.0 copy-start.1
  490.5 11.4 %reshape.21 = bf16[8,160,1,2560]{3,0,1,2:T(8,128)(2,1)} reshape(bf16[2,4,160,1,2560]{4,1,0,2,3:T(4,128)(2,1)} %copy.12) | data formatting | bytes 13107200 | tf_op jit(solution)/shard_map/reshape | solution.py:24
  502.0 0.0 copy-done.2
  502.0 7.4 %fusion.3 = f32[2,160,2560]{2,0,1:T(2,128)S(1)} fusion(bf16[8,160,1,2560]{3,0,1,2:T(8,128)(2,1)} %reshape.21, f32[2,8]{1,0:T(2,128)S(1)} %copy-done.2), kind=kOutput, calls=%fused_computation.4 | convolution fusion | flops 78643200 | bytes 9830464 | tf_op jit(solution)/shard_map/tm,rmc->trc/dot_general | solution.py:56
  509.3 2.3 copy.13
  511.6 0.0 copy-done.1
Async XLA Ops:
  6.5 255.5 %copy-start = (bf16[1,256,4096]{2,1,0:T(8,128)(2,1)S(1)}, bf16[1,256,4096]{2,1,0:T(8,128)(2,1)}, u32[]{:S(2)}) copy-start(bf16[1,256,4096]{2,1,0:T(8,128)(2,1)} %param.4) | copy-start | bytes 6291460
  6.5 229.0 %all-gather.10.cloned.1.call-start = ((), (), s32[]{:S(2)}) async-start(), calls=%async_computation.3 | async-start | bytes 25362432 | tf_op jit(solution)/shard_map/all_gather | solution.py:36
  7.3 254.8 %copy-start.3 = (bf16[2560,256]{1,0:T(8,128)(2,1)S(1)}, bf16[2560,256]{1,0:T(8,128)(2,1)}, u32[]{:S(2)}) copy-start(bf16[2560,256]{1,0:T(8,128)(2,1)} %param.5) | copy-start | bytes 3932164
  7.3 368.4 %reduce-scatter.4.cloned.1.call-start = ((), (), s32[]{:S(2)}) async-start(), calls=%async_computation.4 | async-start | bytes 13926400 | tf_op jit(solution)/shard_map/reduce_scatter | solution.py:47
  296.5 114.7 %all-gather.8.cloned.1.call-start = ((), (), s32[]{:S(2)}) async-start(), calls=%async_computation.2 | async-start | bytes 2457600 | tf_op jit(solution)/shard_map/all_gather | solution.py:20
  375.7 104.2 %all-gather.6.cloned.1.call-start = ((), (), s32[]{:S(2)}) async-start(), calls=%async_computation.1 | async-start | bytes 8192000 | tf_op jit(solution)/shard_map/all_gather | solution.py:20
  490.5 11.4 %copy-start.2 = (f32[2,8]{1,0:T(2,128)S(1)}, f32[2,8]{1,0:T(2,128)}, u32[]{:S(2)}) copy-start(f32[2,8]{1,0:T(2,128)} %param.7) | copy-start | bytes 196
  490.5 21.1 %copy-start.1 = (bf16[1,256,4096]{2,1,0:T(8,128)(2,1)S(1)}, bf16[1,256,4096]{2,1,0:T(8,128)(2,1)}, u32[]{:S(2)}) copy-start(bf16[1,256,4096]{2,1,0:T(8,128)(2,1)} %param.4) | copy-start | bytes 6291460
Sparse Core Ops, SparseCore 0:
  9.1 226.4 all-gather.9
  296.6 79.0 reduce-scatter.3
  377.4 33.7 all-gather.7
  412.7 67.1 all-gather.5
where the time goes:
time: 520 us; the launch traced here: 518 us
  waiting for transfers between devices  412 us (79%)
  local copies, waits for them, and re-layouts  68.5 us (13%)
  matrix products  24.1 us (5%)
  between operations  13.1 us (3%)
    all_gather x1, waiting for transfers between devices, on_device(): lax.all_gather(expand_in, LAYER_WIDTH, axis=0, tiled=True)  228 us
    all_gather x2, waiting for transfers between devices, stacked_from(): parts = lax.all_gather(parts, axes[k], axis=0, tiled=True)  104 us
    reduce_scatter x1, waiting for transfers between devices, on_device(): lax.psum_scatter(partial_value.astype(jnp.float32).reshape(own_rows * lax...  79.2 us
    unnamed x10, local copies, waits for them, and re-layouts  44.1 us
    dot_general x1, matrix products, on_device(): jnp.einsum('ri,kic->rkc', expand_out, projected, preferred_element_type=j...  16.7 us
    reshape x1, local copies, waits for them, and re-layouts, stacked_from(): parts.transpose(*turned, *range(len(order), parts.ndim))  11.4 us
    transpose x1, local copies, waits for them, and re-layouts, stacked_from(): parts.transpose(*turned, *range(len(order), parts.ndim))  10.6 us
  transfers between devices with their start and end apart: 4, of which 4 were waited for; matrix products, arithmetic and copies ran while one was open for 0% of the time, Pallas kernels for 0%

commit v1 on v0

--- a/solution.py
+++ b/solution.py
@@ -6,6 +6,12 @@
 
 LAYER_WIDTH = ("layer_0", "layer_1", "width")
 LAYER = ("layer_0", "layer_1")
+
+
+def _spread_plane(inputs):
+    return jnp.concatenate(
+        lax.all_to_all(jnp.stack([inputs] * lax.axis_size(LAYER_WIDTH), 0), LAYER_WIDTH, 0, 0), 0
+    )
 
 
 def in_order(parts, dim):
@@ -33,7 +39,7 @@
     stacked = source.reshape(src_held * row_count, inner_width)
     projected = lax.dot_general(
         stacked,
-        lax.all_gather(expand_in, LAYER_WIDTH, axis=0, tiled=True),
+        _spread_plane(expand_in),
         (((1,), (1,)), ((), ())),
         preferred_element_type=jnp.float32,
     )

time: 520 us -> 609 us (1.17)
  blocking collectives: 0 us -> 296 us
  waiting for transfers between devices: 412 us -> 200 us
    all_to_all x0 -> x1, blocking collectives: none -> 296 us  [_spread_plane(): lax.all_to_all(jnp.stack([inputs] * lax.axis_size(LAYER_WIDTH), 0), LAYER...]
    all_gather x1 -> x0, waiting for transfers between devices: 228 us -> none  [on_device(): lax.all_gather(expand_in, LAYER_WIDTH, axis=0, tiled=True)]
    reshape x0 -> x1, local copies, waits for them, and re-layouts: none -> 26.6 us  [_spread_plane(): jnp.concatenate(lax.all_to_all(jnp.stack([inputs] * lax.axis_size(LAYER_W...]
    unnamed x10 -> x9, local copies, waits for them, and re-layouts: 44.1 us -> 17.6 us
    reduce_scatter x1, waiting for transfers between devices: 79.2 us -> 96.2 us  [on_device(): lax.psum_scatter(partial_value.astype(jnp.float32).reshape(own_rows * lax...]
  transfers between devices with their start and end apart: 4 -> 3, of which waited for: 4 -> 3; matrix products, arithmetic and copies ran while one was open for 0% -> 0% of each run, Pallas kernels for 0% -> 0%
where the time goes in v1:
time: 609 us; the launch traced here: 607 us
  blocking collectives  296 us (49%)
  waiting for transfers between devices  200 us (33%)
  local copies, waits for them, and re-layouts  73.3 us (12%)
  matrix products  24.1 us (4%)
  between operations  13.1 us (2%)
    all_to_all x1, blocking collectives, _spread_plane(): lax.all_to_all(jnp.stack([inputs] * lax.axis_size(LAYER_WIDTH), 0), LAYER...  296 us
    all_gather x2, waiting for transfers between devices, stacked_from(): parts = lax.all_gather(parts, axes[k], axis=0, tiled=True)  104 us
    reduce_scatter x1, waiting for transfers between devices, on_device(): lax.psum_scatter(partial_value.astype(jnp.float32).reshape(own_rows * lax...  96.2 us
    reshape x1, local copies, waits for them, and re-layouts, _spread_plane(): jnp.concatenate(lax.all_to_all(jnp.stack([inputs] * lax.axis_size(LAYER_W...  26.6 us
    unnamed x9, local copies, waits for them, and re-layouts  17.6 us
    dot_general x1, matrix products, on_device(): jnp.einsum('ri,kic->rkc', expand_out, projected, preferred_element_type=j...  16.7 us
  transfers between devices with their start and end apart: 3, of which 3 were waited for; matrix products, arithmetic and copies ran while one was open for 0% of the time, Pallas kernels for 0%

profile of v1, /device:TPU:1, one launch (start us, length us, event | category | flops | bytes accessed | tf_op | source)
XLA Modules:
  0.0 607.1 jit_solution(10722201076708766691)
XLA Ops:
  6.5 0.0 copy-start
  6.5 0.0 reduce-scatter.4.cloned.1.call-start
  6.5 4.7 stack.2
  11.2 296.0 %all_to_all.5 = bf16[128,20,4096]{2,1,0:T(8,128)(2,1)} all-to-all(bf16[128,20,4096]{2,1,0:T(8,128)(2,1)S(1)} %stack.2), channel_id=1, replica_groups=mesh['layer_0'=2,'layer_1'=4,'width'=16] {'layer_0','layer_1','width'}, dimensions={0} | all-to-all | bytes 41943040 | tf_op jit(solution)/shard_map/all_to_all | solution.py:13
  307.2 0.0 copy-start.3
  307.2 26.6 %reshape.25 = bf16[2560,4096]{1,0:T(8,128)(2,1)} reshape(bf16[128,20,4096]{2,1,0:T(8,128)(2,1)} %all_to_all.5) | data formatting | bytes 41943040 | tf_op jit(solution)/shard_map/reshape | solution.py:12
  333.8 0.0 copy-done
  333.8 0.0 copy-done.3
  333.8 16.7 %fusion = bf16[2560,1,2560]{0,2,1:T(8,128)(2,1)} fusion(bf16[2560,256]{1,0:T(8,128)(2,1)S(1)} %copy-done.3, bf16[2560,4096]{1,0:T(8,128)(2,1)} %reshape.25, bf16[1,256,4096]{2,1,0:T(8,128)(2,1)S(1)} %copy-done), kind=kOutput, calls=%fused_computation.1 | convolution fusion | flops 8731361280 | bytes 37486592 | tf_op jit(solution)/shard_map/ri,kic->rkc/dot_general | solution.py:49
  350.6 17.6 %copy.14 = bf16[2560,2560]{1,0:T(8,128)(2,1)} copy(bf16[2560,2560]{0,1:T(8,128)(2,1)} %bitcast.33) | data formatting | bytes 26214400
  368.2 0.0 reduce-scatter.4.cloned.1.call-update
  368.2 0.0 all-gather.6.cloned.1.call-start
  368.3 96.2 %reduce-scatter.4.cloned.1.call-done = bf16[160,2560]{1,0:T(8,128)(2,1)} async-done(((bf16[2560,2560]{1,0:T(8,128)(2,1)}), bf16[160,2560]{1,0:T(8,128)(2,1)}) %reduce-scatter.4.cloned.1.call-update) | async-done | bytes 819216 | tf_op jit(solution)/shard_map/reduce_scatter | solution.py:53
  464.5 0.0 all-gather.6.cloned.1.call-update
  464.5 0.2 all-gather.4.cloned.1.call-start
  464.7 35.2 %all-gather.6.cloned.1.call-done = bf16[320,2560]{1,0:T(8,128)(2,1)} async-done(((bf16[160,2560]{1,0:T(8,128)(2,1)}), bf16[320,2560]{1,0:T(8,128)(2,1)}) %all-gather.6.cloned.1.call-update) | async-done | bytes 1638416 | tf_op jit(solution)/shard_map/all_gather | solution.py:26
  499.9 0.0 all-gather.4.cloned.1.call-update
  500.0 68.9 %all-gather.4.cloned.1.call-done = bf16[8,160,1,2560]{3,1,2,0:T(8,128)(2,1)} async-done(((bf16[2,160,1,2560]{3,1,2,0:T(8,128)(2,1)}), bf16[8,160,1,2560]{3,1,2,0:T(8,128)(2,1)}) %all-gather.4.cloned.1.call-update) | async-done | bytes 6553616 | tf_op jit(solution)/shard_map/all_gather | solution.py:26
  568.8 10.6 %copy.12 = bf16[2,4,160,1,2560]{4,1,0,2,3:T(4,128)(2,1)} copy(bf16[2,4,160,1,2560]{4,2,0,1,3:T(8,128)(2,1)} %bitcast.34) | data formatting | bytes 13107200 | tf_op jit(solution)/shard_map/transpose | solution.py:30
  579.5 0.0 copy-start.2
  579.5 0.0 copy-start.1
  579.5 11.4 %reshape.27 = bf16[8,160,1,2560]{3,0,1,2:T(8,128)(2,1)} reshape(bf16[2,4,160,1,2560]{4,1,0,2,3:T(4,128)(2,1)} %copy.12) | data formatting | bytes 13107200 | tf_op jit(solution)/shard_map/reshape | solution.py:30
  590.9 0.0 copy-done.2
  590.9 7.4 %fusion.3 = f32[2,160,2560]{2,0,1:T(2,128)S(1)} fusion(bf16[8,160,1,2560]{3,0,1,2:T(8,128)(2,1)} %reshape.27, f32[2,8]{1,0:T(2,128)S(1)} %copy-done.2), kind=kOutput, calls=%fused_computation.4 | convolution fusion | flops 78643200 | bytes 9830464 | tf_op jit(solution)/shard_map/tm,rmc->trc/dot_general | solution.py:62
  598.3 2.3 copy.13
  600.6 0.0 copy-done.1
Async XLA Ops:
  6.5 327.3 %copy-start = (bf16[1,256,4096]{2,1,0:T(8,128)(2,1)S(1)}, bf16[1,256,4096]{2,1,0:T(8,128)(2,1)}, u32[]{:S(2)}) copy-start(bf16[1,256,4096]{2,1,0:T(8,128)(2,1)} %param.4) | copy-start | bytes 6291460
  6.5 457.9 %reduce-scatter.4.cloned.1.call-start = ((), (), s32[]{:S(2)}) async-start(), calls=%async_computation.4 | async-start | bytes 13926400 | tf_op jit(solution)/shard_map/reduce_scatter | solution.py:53
  307.2 26.6 %copy-start.3 = (bf16[2560,256]{1,0:T(8,128)(2,1)S(1)}, bf16[2560,256]{1,0:T(8,128)(2,1)}, u32[]{:S(2)}) copy-start(bf16[2560,256]{1,0:T(8,128)(2,1)} %param.5) | copy-start | bytes 3932164
  368.2 131.7 %all-gather.6.cloned.1.call-start = ((), (), s32[]{:S(2)}) async-start(), calls=%async_computation.3 | async-start | bytes 2457600 | tf_op jit(solution)/shard_map/all_gather | solution.py:26
  464.5 104.3 %all-gather.4.cloned.1.call-start = ((), (), s32[]{:S(2)}) async-start(), calls=%async_computation.2 | async-start | bytes 8192000 | tf_op jit(solution)/shard_map/all_gather | solution.py:26
  579.5 11.4 %copy-start.2 = (f32[2,8]{1,0:T(2,128)S(1)}, f32[2,8]{1,0:T(2,128)}, u32[]{:S(2)}) copy-start(f32[2,8]{1,0:T(2,128)} %param.7) | copy-start | bytes 196
  579.5 21.1 %copy-start.1 = (bf16[1,256,4096]{2,1,0:T(8,128)(2,1)S(1)}, bf16[1,256,4096]{2,1,0:T(8,128)(2,1)}, u32[]{:S(2)}) copy-start(bf16[1,256,4096]{2,1,0:T(8,128)(2,1)} %param.4) | copy-start | bytes 6291460
Sparse Core Ops, SparseCore 0:
  368.4 96.0 reduce-scatter.3
  466.1 33.7 all-gather.5
  501.6 67.1 all-gather.3
